TPU v7x, 32 devices: a whole 2x2x4 slice. The times are simulated.
32 devices in a mesh: bank: 4 (over z), zero: 8 (over y, x, core).
Axes of the slice: x: 2, y: 2, z: 4, core: 2. Of those that a mesh axis runs over, the one named last changes fastest.
Arguments:
- train_gate: float32 [64, 2048, 1408], P('bank', 'zero'), may hold values from -0.1875 to 0.1875
- train_up: float32 [64, 2048, 1408], P('bank', 'zero'), may hold values from -0.1875 to 0.1875
- router_weight: float32 [2048, 64], P('zero', 'bank'), may hold values from -0.125 to 0.125
- router_gain: float32 [2048], P('zero'), may hold values from 0.25 to 1.75
Outputs:
- ready_gate: bfloat16 [64, 2048, 1408], P('bank', None, 'zero')
- ready_up: bfloat16 [64, 2048, 1408], P('bank', None, 'zero')
- scale_gate: float32 [64, 1408], P('bank', 'zero')
- scale_up: float32 [64, 1408], P('bank', 'zero')
- serve_router: bfloat16 [2048, 64], replicated
All inputs are finite; a program needn't handle non-finite values. Where the computation divides by a largest or mean magnitude, that divisor is 1e-20 or more.
Results may differ from a plain program's by a relative error of at most 0.012.
Values may be sent and summed in bfloat16 or wider, within the bound.
A program may use at most 192 MiB of HBM per device.

v0:
```python
import functools

import jax
import jax.numpy as jnp
from jax import lax
from jax.experimental import pallas as pl
from jax.experimental.pallas import tpu as pltpu
from jax.sharding import PartitionSpec as P

MESH = pl.DeviceIdType.MESH
LANES = 128
SLOTS = 8
LAG = 5
KERNEL_VMEM = 28 * 2**20
FINISH_VMEM = 2 * 2**20


def exchange(
    n, nb, gate, up, weight, gain, recv, router, scale_gate, scale_up, inbuf, turned, send, part, wide,
    in_sem, send_sem, recv_sem, bank_send, bank_recv, zero_send, zero_recv,
):
    experts, rows, cols = gate.shape
    width = cols // n
    steps = 2 * experts
    slots = send.shape[0]
    lag = min(LAG, experts)
    me = lax.axis_index("zero")
    bank = lax.axis_index("bank")

    def fetch(source, e, slot):
        return pltpu.make_async_copy(source.at[e], inbuf.at[slot], in_sem.at[slot])

    fetch(gate, 0, 0).start()
    fetch(up, 0, 1).start()

    barrier = pltpu.get_barrier_semaphore()
    for k in range(1, n):
        pl.semaphore_signal(barrier, inc=1, device_id={"zero": lax.rem(me + k, n)}, device_id_type=MESH)
    for k in range(1, nb):
        pl.semaphore_signal(barrier, inc=1, device_id={"bank": lax.rem(bank + k, nb)}, device_id_type=MESH)
    scale_gate[...] = jnp.zeros_like(scale_gate)
    scale_up[...] = jnp.zeros_like(scale_up)
    part[...] = (weight[...] * gain[...]).astype(part.dtype)

    def peer_copy(half, e, slot, k):
        peer = lax.rem(me + k, n)
        return pltpu.make_async_remote_copy(
            src_ref=send.at[slot, peer],
            dst_ref=recv.at[me, half, e],
            send_sem=send_sem.at[slot, k],
            recv_sem=recv_sem.at[e, k],
            device_id={"zero": peer},
            device_id_type=MESH,
        )

    def turn(half, slot):
        for j in range(0, cols, LANES):
            turned[j : j + LANES, :] = inbuf[half, :, j : j + LANES].T
        for d in range(n):
            send[slot, d] = turned[d * width : (d + 1) * width, :].astype(send.dtype)

    def drain(slot):
        for k in range(1, n):
            peer_copy(0, 0, slot, k).wait_send()

    def launch(half, e, slot):
        for k in range(1, n):
            peer_copy(half, e, slot, k).start()
        recv[me, half, e] = send[slot, me]

    def settle(e):
        for k in range(1, n):
            source = lax.rem(me - k + n, n)
            pltpu.make_async_remote_copy(
                src_ref=recv.at[source, :, e],
                dst_ref=recv.at[source, :, e],
                send_sem=send_sem.at[0, 0],
                recv_sem=recv_sem.at[e, k],
                device_id={"zero": source},
                device_id_type=MESH,
            ).wait_recv()
        for half, scale in enumerate((scale_gate, scale_up)):
            total = jnp.zeros((width, LANES), jnp.float32)
            for s in range(n):
                for j in range(0, rows, LANES):
                    total += jnp.abs(recv[s, half, e, :, j : j + LANES].astype(jnp.float32))
            mean = jnp.sum(total, axis=1, keepdims=True) / (rows * n)
            wide[0:width, :] = jnp.broadcast_to(mean, (width, LANES))
            for j in range(0, width, LANES):
                stop = min(j + LANES, width)
                line = wide[j : j + LANES, :].T[0:1, 0 : stop - j]
                here = lax.broadcasted_iota(jnp.int32, (experts, stop - j), 0) == e
                scale[:, j:stop] = jnp.where(here, line, scale[:, j:stop])
            inverse = jnp.broadcast_to(1.0 / mean, (width, LANES))
            for s in range(n):
                for j in range(0, rows, LANES):
                    value = recv[s, half, e, :, j : j + LANES].astype(jnp.float32) * inverse
                    recv[s, half, e, :, j : j + LANES] = value.astype(recv.dtype)

    def column(z):
        return pl.ds(pl.multiple_of(z * rows, rows), rows)

    def bank_copy(k):
        return pltpu.make_async_remote_copy(
            src_ref=part,
            dst_ref=router.at[bank, :, column(me)],
            send_sem=bank_send.at[k],
            recv_sem=bank_recv.at[k],
            device_id={"bank": lax.rem(bank + k, nb)},
            device_id_type=MESH,
        )

    def zero_copy(k):
        return pltpu.make_async_remote_copy(
            src_ref=router.at[:, :, column(me)],
            dst_ref=router.at[:, :, column(me)],
            send_sem=zero_send.at[k],
            recv_sem=zero_recv.at[k],
            device_id={"zero": lax.rem(me + k, n)},
            device_id_type=MESH,
        )

    fetch(gate, 0, 0).wait()
    turn(0, 0)
    pl.semaphore_wait(barrier, n - 1 + nb - 1)

    router[bank, :, column(me)] = part[...]
    for k in range(1, nb):
        bank_copy(k).start()

    @pl.loop(0, experts)
    def _(e):
        for half, source in enumerate((gate, up)):
            t = 2 * e + half
            slot = lax.rem(t, slots)

            def ready():
                fetch(source, e, half).wait()

                @pl.when(t >= slots)
                def _():
                    drain(slot)

                turn(half, slot)

            if half == 0:
                pl.when(e > 0)(ready)
            else:
                ready()
            launch(half, e, slot)

            @pl.when(e + 1 < experts)
            def _():
                fetch(source, e + 1, half).start()

        @pl.when(e == min(1, experts - 1))
        def _():
            for k in range(1, nb):
                bank_copy(k).wait()
            for k in range(1, n):
                zero_copy(k).start()

        @pl.when(e >= lag)
        def _():
            settle(e - lag)

    @pl.loop(experts - lag, experts)
    def _(e):
        settle(e)

    for k in range(1, n):
        zero_copy(k).wait()

    @pl.loop(max(steps - slots, 0), steps)
    def _(t):
        drain(lax.rem(t, slots))


def finish(
    recv, router, scale_gate, scale_up,
    ready_gate, ready_up, router_out, scale_gate_out, scale_up_out, sem, router_sem,
):
    n, rows = recv.shape[0], recv.shape[4]
    copies = [
        pltpu.make_async_copy(recv.at[s, half], ready.at[:, :, s * rows : (s + 1) * rows], sem.at[s, half])
        for s in range(n)
        for half, ready in enumerate((ready_gate, ready_up))
    ]
    copies.append(pltpu.make_async_copy(router, router_out, router_sem))
    for copy in copies:
        copy.start()
    scale_gate_out[...] = scale_gate[...]
    scale_up_out[...] = scale_up[...]
    for copy in copies:
        copy.wait()


def solution(mesh):
    n, nb = mesh.shape["zero"], mesh.shape["bank"]

    def local(train_gate, train_up, router_weight, router_gain):
        experts, rows, cols = train_gate.shape
        width = cols // n
        d_model = rows * n
        mine = router_weight.shape[1]
        slots = min(SLOTS, 2 * experts)
        anywhere = pl.BlockSpec(memory_space=pl.ANY)
        inside = pl.BlockSpec(memory_space=pltpu.VMEM)
        padded = -(-width // LANES) * LANES
        scale = jax.ShapeDtypeStruct((experts, width), jnp.float32)
        joined = jax.ShapeDtypeStruct((nb, mine, d_model), jnp.bfloat16)
        recv, router, scale_gate, scale_up = pl.pallas_call(
            functools.partial(exchange, n, nb),
            out_shape=(
                jax.ShapeDtypeStruct((n, 2, experts, width, rows), jnp.bfloat16),
                joined,
                scale,
                scale,
            ),
            in_specs=[anywhere, anywhere, inside, inside],
            out_specs=(inside,) * 4,
            scratch_shapes=[
                pltpu.VMEM((2, rows, cols), jnp.float32),
                pltpu.VMEM((cols, rows), jnp.float32),
                pltpu.VMEM((slots, n, width, rows), jnp.bfloat16),
                pltpu.VMEM((mine, rows), jnp.bfloat16),
                pltpu.VMEM((padded, LANES), jnp.float32),
                pltpu.SemaphoreType.DMA((2,)),
                pltpu.SemaphoreType.DMA((slots, n)),
                pltpu.SemaphoreType.DMA((experts, n)),
                pltpu.SemaphoreType.DMA((nb,)),
                pltpu.SemaphoreType.DMA((nb,)),
                pltpu.SemaphoreType.DMA((n,)),
                pltpu.SemaphoreType.DMA((n,)),
            ],
            compiler_params=pltpu.CompilerParams(
                collective_id=0, has_side_effects=True, vmem_limit_bytes=KERNEL_VMEM
            ),
        )(train_gate, train_up, router_weight.T, router_gain[None, :])

        ready = jax.ShapeDtypeStruct((experts, width, d_model), jnp.bfloat16)
        ready_gate, ready_up, router, scale_gate, scale_up = pl.pallas_call(
            finish,
            out_shape=(ready, ready, joined, scale, scale),
            in_specs=[inside] * 4,
            out_specs=(anywhere, anywhere, anywhere, inside, inside),
            scratch_shapes=[pltpu.SemaphoreType.DMA((n, 2)), pltpu.SemaphoreType.DMA],
            compiler_params=pltpu.CompilerParams(vmem_limit_bytes=FINISH_VMEM),
        )(recv, router, scale_gate, scale_up)
        return (
            jnp.swapaxes(ready_gate, 1, 2),
            jnp.swapaxes(ready_up, 1, 2),
            scale_gate,
            scale_up,
            router.reshape(nb * mine, d_model).T,
        )

    in_specs = (P("bank", "zero", None), P("bank", "zero", None), P("zero", "bank"), P("zero"))
    out_specs = (
        P("bank", None, "zero"),
        P("bank", None, "zero"),
        P("bank", "zero"),
        P("bank", "zero"),
        P(),
    )
    return jax.shard_map(local, mesh=mesh, in_specs=in_specs, out_specs=out_specs, check_vma=False)
```

profile of v0, /device:TPU:1, one launch (start us, length us, event | category | flops | bytes accessed | tf_op | source)
XLA Modules:
  0.0 271.0 jit_solution(7875785527792231013)
XLA Ops:
  0.6 0.0 copy-start
  0.6 0.7 copy-done
  1.4 0.0 copy-start.1
  1.4 0.7 copy-done.1
  2.0 260.4 %shard_map.83 = (bf16[8,2,16,176,256]{4,3,2,1,0:T(8,128)(2,1)S(1)}, bf16[4,16,2048]{2,1,0:T(8,128)(2,1)S(1)}, f32[16,176]{1,0:T(8,128)S(1)}, f32[16,176]{1,0:T(8,128)S(1)}) custom-call(f32[16,256,1408]{2,1,0:T(8,128)} %gate.1, f32[16,256,1408]{2,1,0:T(8,128)} %up.1, f32[16,256]{1,0:T(8,128)S(1)} %bitcast.7, f32[1,256]{1,0:T(1,128)S(1)} %bitcast.8), custom_call_target="tpu_custom_call" | custom-call | tf_op jit(solution)/shard_map/pallas_call | solution.py:212
  262.4 8.5 %shard_map.84 = (bf16[16,176,2048]{2,1,0:T(8,128)(2,1)}, bf16[16,176,2048]{2,1,0:T(8,128)(2,1)}, bf16[4,16,2048]{2,1,0:T(8,128)(2,1)}, f32[16,176]{1,0:T(8,128)}, f32[16,176]{1,0:T(8,128)}) custom-call(bf16[8,2,16,176,256]{4,3,2,1,0:T(8,128)(2,1)S(1)} %get-tuple-element.14.recv, bf16[4,16,2048]{2,1,0:T(8,128)(2,1)S(1)} %get-tuple-element.15.router, ...), custom_call_target="tpu_custom_call" | custom-call | tf_op jit(solution)/shard_map/pallas_call | solution.py:242
Async XLA Ops:
  0.6 0.7 copy-start
  1.4 0.7 copy-start.1
where the time goes:
time: 271 us
  Pallas kernels  269 us (99%)
    pallas_call x1, Pallas kernels, local(): pl.pallas_call(functools.partial(exchange, n, nb), out_shape=(jax.ShapeDt...  260 us
    pallas_call x1, Pallas kernels, local(): pl.pallas_call(finish, out_shape=(ready, ready, joined, scale, scale), in...  8.52 us

commit v1 on v0

--- a/solution.py
+++ b/solution.py
@@ -17,7 +17,7 @@
 
 def exchange(
     n, nb, gate, up, weight, gain, recv, router, scale_gate, scale_up, inbuf, turned, send, part, wide,
-    in_sem, send_sem, recv_sem, bank_send, bank_recv, zero_send, zero_recv,
+    weight_buf, gain_buf, in_sem, router_sem, send_sem, recv_sem, bank_send, bank_recv, zero_send, zero_recv,
 ):
     experts, rows, cols = gate.shape
     width = cols // n
@@ -30,7 +30,14 @@
     def fetch(source, e, slot):
         return pltpu.make_async_copy(source.at[e], inbuf.at[slot], in_sem.at[slot])
 
+    router_in = (
+        pltpu.make_async_copy(weight, weight_buf, router_sem.at[0]),
+        pltpu.make_async_copy(gain, gain_buf, router_sem.at[1]),
+    )
+
     fetch(gate, 0, 0).start()
+    for copy in router_in:
+        copy.start()
     fetch(up, 0, 1).start()
 
     barrier = pltpu.get_barrier_semaphore()
@@ -40,7 +47,6 @@
         pl.semaphore_signal(barrier, inc=1, device_id={"bank": lax.rem(bank + k, nb)}, device_id_type=MESH)
     scale_gate[...] = jnp.zeros_like(scale_gate)
     scale_up[...] = jnp.zeros_like(scale_up)
-    part[...] = (weight[...] * gain[...]).astype(part.dtype)
 
     def peer_copy(half, e, slot, k):
         peer = lax.rem(me + k, n)
@@ -48,7 +54,7 @@
             src_ref=send.at[slot, peer],
             dst_ref=recv.at[me, half, e],
             send_sem=send_sem.at[slot, k],
-            recv_sem=recv_sem.at[e, k],
+            recv_sem=recv_sem.at[2 * e + half, k],
             device_id={"zero": peer},
             device_id_type=MESH,
         )
@@ -68,34 +74,38 @@
             peer_copy(half, e, slot, k).start()
         recv[me, half, e] = send[slot, me]
 
-    def settle(e):
-        for k in range(1, n):
+    def settle(half, scale, e):
+        total = jnp.zeros((width, LANES), jnp.float32)
+        for k in range(n):
             source = lax.rem(me - k + n, n)
-            pltpu.make_async_remote_copy(
-                src_ref=recv.at[source, :, e],
-                dst_ref=recv.at[source, :, e],
-                send_sem=send_sem.at[0, 0],
-                recv_sem=recv_sem.at[e, k],
-                device_id={"zero": source},
-                device_id_type=MESH,
-            ).wait_recv()
+            block = recv.at[source, half, e]
+            if k > 0:
+                pltpu.make_async_remote_copy(
+                    src_ref=block,
+                    dst_ref=block,
+                    send_sem=send_sem.at[0, 0],
+                    recv_sem=recv_sem.at[2 * e + half, k],
+                    device_id={"zero": source},
+                    device_id_type=MESH,
+                ).wait_recv()
+            for j in range(0, rows, LANES):
+                total += jnp.abs(block[:, j : j + LANES].astype(jnp.float32))
+        mean = jnp.sum(total, axis=1, keepdims=True) / (rows * n)
+        wide[0:width, :] = jnp.broadcast_to(mean, (width, LANES))
+        for j in range(0, width, LANES):
+            stop = min(j + LANES, width)
+            line = wide[j : j + LANES, :].T[0:1, 0 : stop - j]
+            here = lax.broadcasted_iota(jnp.int32, (experts, stop - j), 0) == e
+            scale[:, j:stop] = jnp.where(here, line, scale[:, j:stop])
+        inverse = jnp.broadcast_to(1.0 / mean, (width, LANES))
+        for s in range(n):
+            for j in range(0, rows, LANES):
+                value = recv[s, half, e, :, j : j + LANES].astype(jnp.float32) * inverse
+                recv[s, half, e, :, j : j + LANES] = value.astype(recv.dtype)
+
+    def settle_both(e):
         for half, scale in enumerate((scale_gate, scale_up)):
-            total = jnp.zeros((width, LANES), jnp.float32)
-            for s in range(n):
-                for j in range(0, rows, LANES):
-                    total += jnp.abs(recv[s, half, e, :, j : j + LANES].astype(jnp.float32))
-            mean = jnp.sum(total, axis=1, keepdims=True) / (rows * n)
-            wide[0:width, :] = jnp.broadcast_to(mean, (width, LANES))
-            for j in range(0, width, LANES):
-                stop = min(j + LANES, width)
-                line = wide[j : j + LANES, :].T[0:1, 0 : stop - j]
-                here = lax.broadcasted_iota(jnp.int32, (experts, stop - j), 0) == e
-                scale[:, j:stop] = jnp.where(here, line, scale[:, j:stop])
-            inverse = jnp.broadcast_to(1.0 / mean, (width, LANES))
-            for s in range(n):
-                for j in range(0, rows, LANES):
-                    value = recv[s, half, e, :, j : j + LANES].astype(jnp.float32) * inverse
-                    recv[s, half, e, :, j : j + LANES] = value.astype(recv.dtype)
+            settle(half, scale, e)
 
     def column(z):
         return pl.ds(pl.multiple_of(z * rows, rows), rows)
@@ -124,6 +134,11 @@
     turn(0, 0)
     pl.semaphore_wait(barrier, n - 1 + nb - 1)
 
+    launch(0, 0, 0)
+
+    for copy in router_in:
+        copy.wait()
+    part[...] = (weight_buf[...] * gain_buf[...]).astype(part.dtype)
     router[bank, :, column(me)] = part[...]
     for k in range(1, nb):
         bank_copy(k).start()
@@ -143,11 +158,12 @@
 
                 turn(half, slot)
 
+                launch(half, e, slot)
+
             if half == 0:
                 pl.when(e > 0)(ready)
             else:
                 ready()
-            launch(half, e, slot)
 
             @pl.when(e + 1 < experts)
             def _():
@@ -162,11 +178,11 @@
 
         @pl.when(e >= lag)
         def _():
-            settle(e - lag)
+            settle_both(e - lag)
 
     @pl.loop(experts - lag, experts)
     def _(e):
-        settle(e)
+        settle_both(e)
 
     for k in range(1, n):
         zero_copy(k).wait()
@@ -178,7 +194,7 @@
 
 def finish(
     recv, router, scale_gate, scale_up,
-    ready_gate, ready_up, router_out, scale_gate_out, scale_up_out, sem, router_sem,
+    ready_gate, ready_up, router_out, scale_gate_out, scale_up_out, sem, small_sem,
 ):
     n, rows = recv.shape[0], recv.shape[4]
     copies = [
@@ -186,11 +202,13 @@
         for s in range(n)
         for half, ready in enumerate((ready_gate, ready_up))
     ]
-    copies.append(pltpu.make_async_copy(router, router_out, router_sem))
+    copies += [
+        pltpu.make_async_copy(router, router_out, small_sem.at[0]),
+        pltpu.make_async_copy(scale_gate, scale_gate_out, small_sem.at[1]),
+        pltpu.make_async_copy(scale_up, scale_up_out, small_sem.at[2]),
+    ]
     for copy in copies:
         copy.start()
-    scale_gate_out[...] = scale_gate[...]
-    scale_up_out[...] = scale_up[...]
     for copy in copies:
         copy.wait()
 
@@ -204,7 +222,7 @@
         d_model = rows * n
         mine = router_weight.shape[1]
         slots = min(SLOTS, 2 * experts)
-        anywhere = pl.BlockSpec(memory_space=pl.ANY)
+        hbm = pl.BlockSpec(memory_space=pltpu.HBM)
         inside = pl.BlockSpec(memory_space=pltpu.VMEM)
         padded = -(-width // LANES) * LANES
         scale = jax.ShapeDtypeStruct((experts, width), jnp.float32)
@@ -217,7 +235,7 @@
                 scale,
                 scale,
             ),
-            in_specs=[anywhere, anywhere, inside, inside],
+            in_specs=[hbm] * 4,
             out_specs=(inside,) * 4,
             scratch_shapes=[
                 pltpu.VMEM((2, rows, cols), jnp.float32),
@@ -225,9 +243,12 @@
                 pltpu.VMEM((slots, n, width, rows), jnp.bfloat16),
                 pltpu.VMEM((mine, rows), jnp.bfloat16),
                 pltpu.VMEM((padded, LANES), jnp.float32),
+                pltpu.VMEM((mine, rows), jnp.float32),
+                pltpu.VMEM((1, rows), jnp.float32),
+                pltpu.SemaphoreType.DMA((2,)),
                 pltpu.SemaphoreType.DMA((2,)),
                 pltpu.SemaphoreType.DMA((slots, n)),
-                pltpu.SemaphoreType.DMA((experts, n)),
+                pltpu.SemaphoreType.DMA((2 * experts, n)),
                 pltpu.SemaphoreType.DMA((nb,)),
                 pltpu.SemaphoreType.DMA((nb,)),
                 pltpu.SemaphoreType.DMA((n,)),
@@ -236,15 +257,20 @@
             compiler_params=pltpu.CompilerParams(
                 collective_id=0, has_side_effects=True, vmem_limit_bytes=KERNEL_VMEM
             ),
-        )(train_gate, train_up, router_weight.T, router_gain[None, :])
+        )(
+            train_gate,
+            train_up,
+            pltpu.with_memory_space_constraint(router_weight.T, pltpu.HBM),
+            pltpu.with_memory_space_constraint(router_gain[None, :], pltpu.HBM),
+        )
 
         ready = jax.ShapeDtypeStruct((experts, width, d_model), jnp.bfloat16)
         ready_gate, ready_up, router, scale_gate, scale_up = pl.pallas_call(
             finish,
             out_shape=(ready, ready, joined, scale, scale),
             in_specs=[inside] * 4,
-            out_specs=(anywhere, anywhere, anywhere, inside, inside),
-            scratch_shapes=[pltpu.SemaphoreType.DMA((n, 2)), pltpu.SemaphoreType.DMA],
+            out_specs=(hbm,) * 5,
+            scratch_shapes=[pltpu.SemaphoreType.DMA((n, 2)), pltpu.SemaphoreType.DMA((3,))],
             compiler_params=pltpu.CompilerParams(vmem_limit_bytes=FINISH_VMEM),
         )(recv, router, scale_gate, scale_up)
         return (

time: 271 us -> 270 us (level)
  no operation moved by 1% of the time
where the time goes in v1:
time: 270 us
  Pallas kernels  269 us (100%)
    pallas_call x1, Pallas kernels, local(): pl.pallas_call(functools.partial(exchange, n, nb), out_shape=(jax.ShapeDt...  261 us
    pallas_call x1, Pallas kernels, local(): pl.pallas_call(finish, out_shape=(ready, ready, joined, scale, scale), in...  7.98 us

profile of v1, /device:TPU:1, one launch (start us, length us, event | category | flops | bytes accessed | tf_op | source)
XLA Modules:
  0.0 269.9 jit_solution(8774917448598143986)
XLA Ops:
  0.6 261.2 %shard_map.83 = (bf16[8,2,16,176,256]{4,3,2,1,0:T(8,128)(2,1)S(1)}, bf16[4,16,2048]{2,1,0:T(8,128)(2,1)S(1)}, f32[16,176]{1,0:T(8,128)S(1)}, f32[16,176]{1,0:T(8,128)S(1)}) custom-call(f32[16,256,1408]{2,1,0:T(8,128)} %gate.1, f32[16,256,1408]{2,1,0:T(8,128)} %up.1, f32[16,256]{1,0:T(8,128)} %bitcast.7, f32[1,256]{1,0:T(1,128)} %bitcast.8), custom_call_target="tpu_custom_call" | custom-call | tf_op jit(solution)/shard_map/pallas_call | solution.py:230
  261.9 8.0 %shard_map.84 = (bf16[16,176,2048]{2,1,0:T(8,128)(2,1)}, bf16[16,176,2048]{2,1,0:T(8,128)(2,1)}, bf16[4,16,2048]{2,1,0:T(8,128)(2,1)}, f32[16,176]{1,0:T(8,128)}, f32[16,176]{1,0:T(8,128)}) custom-call(bf16[8,2,16,176,256]{4,3,2,1,0:T(8,128)(2,1)S(1)} %get-tuple-element.14.recv, bf16[4,16,2048]{2,1,0:T(8,128)(2,1)S(1)} %get-tuple-element.15.router, ...), custom_call_target="tpu_custom_call" | custom-call | tf_op jit(solution)/shard_map/pallas_call | solution.py:268

commit v2 on v1

v2 whole, which is shorter than its diff:
```python
import functools

import jax
import jax.numpy as jnp
from jax import lax
from jax.experimental import pallas as pl
from jax.experimental.pallas import tpu as pltpu
from jax.sharding import PartitionSpec as P

MESH = pl.DeviceIdType.MESH
LANES = 128
SLOTS = 8
LAG = 5
TAIL = 3 / 16
EXCHANGE_VMEM = 28 * 2**20
CROSS_VMEM = 8 * 2**20
FINISH_VMEM = 2 * 2**20


def at(axis, index):
    return dict(device_id={axis: index}, device_id_type=MESH)


def spread(mean, wide, scale, row):
    width = mean.shape[0]
    wide[0:width, :] = jnp.broadcast_to(mean, (width, LANES))
    for j in range(0, width, LANES):
        stop = min(j + LANES, width)
        line = wide[j : j + LANES, :].T[0:1, 0 : stop - j]
        here = lax.broadcasted_iota(jnp.int32, (scale.shape[0], stop - j), 0) == row
        scale[:, j:stop] = jnp.where(here, line, scale[:, j:stop])


def settle(n, blocks, arrive, wide, scale, row):
    width, rows = blocks(0).shape
    total = jnp.zeros((width, LANES), jnp.float32)
    for k in range(n):
        arrive(k)
        block = blocks(k)
        for j in range(0, rows, LANES):
            total += jnp.abs(block[:, j : j + LANES].astype(jnp.float32))
    mean = jnp.sum(total, axis=1, keepdims=True) / (rows * n)
    inverse = jnp.broadcast_to(1.0 / mean, (width, LANES))
    for k in range(n):
        block = blocks(k)
        for j in range(0, rows, LANES):
            value = block[:, j : j + LANES].astype(jnp.float32) * inverse
            block[:, j : j + LANES] = value.astype(block.dtype)
    spread(mean, wide, scale, row)


def exchange(
    n, nb, gate, up, weight, gain, recv, router, scale_gate, scale_up, late, early,
    inbuf, turned, send, part, wide, weight_buf, gain_buf,
    in_sem, router_sem, send_sem, recv_sem, late_send, late_recv,
    bank_send, bank_recv, zero_send, zero_recv, here_sem, go_sem,
):
    experts, rows, cols = gate.shape
    width = cols // n
    bulk = recv.shape[2]
    slots = send.shape[0]
    lag = min(LAG, bulk)
    me = lax.axis_index("zero")
    bank = lax.axis_index("bank")
    odd = lax.rem(me, 2) == 1

    def fetch(source, e, slot):
        return pltpu.make_async_copy(source.at[e], inbuf.at[slot], in_sem.at[slot])

    router_in = (
        pltpu.make_async_copy(weight, weight_buf, router_sem.at[0]),
        pltpu.make_async_copy(gain, gain_buf, router_sem.at[1]),
    )

    fetch(gate, 0, 0).start()

    barrier = pltpu.get_barrier_semaphore()
    for k in range(1, n):
        peer = lax.rem(me + k, n)

        @pl.when(peer != 0)
        def _():
            pl.semaphore_signal(barrier, inc=1, **at("zero", peer))

    for copy in router_in:
        copy.start()
    scale_gate[...] = jnp.zeros_like(scale_gate)
    scale_up[...] = jnp.zeros_like(scale_up)

    def peer_copy(half, e, slot, k):
        peer = lax.rem(me + k, n)
        return pltpu.make_async_remote_copy(
            src_ref=send.at[slot, peer],
            dst_ref=recv.at[me, half, e],
            send_sem=send_sem.at[slot, k],
            recv_sem=recv_sem.at[2 * e + half, k],
            **at("zero", peer),
        )

    def late_copy(half, e, k):
        peer = lax.rem(me + k, n)
        return pltpu.make_async_remote_copy(
            src_ref=late.at[peer, half, e],
            dst_ref=early.at[me // 2, half, e],
            send_sem=late_send.at[2 * e + half, k],
            recv_sem=late_recv.at[2 * e + half, k],
            **at("zero", peer),
        )

    def turn(half, target):
        for j in range(0, cols, LANES):
            turned[j : j + LANES, :] = inbuf[half, :, j : j + LANES].T
        for d in range(n):
            target(d)[...] = turned[d * width : (d + 1) * width, :].astype(send.dtype)

    def drain(slot):
        for k in range(1, n):
            peer_copy(0, 0, slot, k).wait_send()

    def launch(half, e, slot):
        for k in range(1, n):
            peer_copy(half, e, slot, k).start()
        recv[me, half, e] = send[slot, me]

    def settle_both(e):
        for half, scale in enumerate((scale_gate, scale_up)):

            def block(k):
                return recv.at[lax.rem(me - k + n, n), half, e]

            def arrive(k):
                if k > 0:
                    pltpu.make_async_remote_copy(
                        src_ref=block(k),
                        dst_ref=block(k),
                        send_sem=send_sem.at[0, 0],
                        recv_sem=recv_sem.at[2 * e + half, k],
                        **at("zero", lax.rem(me - k + n, n)),
                    ).wait_recv()

            settle(n, block, arrive, wide, scale, e)

    def column(z):
        return pl.ds(pl.multiple_of(z * rows, rows), rows)

    def bank_copy(k):
        return pltpu.make_async_remote_copy(
            src_ref=part,
            dst_ref=router.at[bank, :, column(me)],
            send_sem=bank_send.at[k],
            recv_sem=bank_recv.at[k],
            **at("bank", lax.rem(bank + k, nb)),
        )

    def zero_copy(k):
        return pltpu.make_async_remote_copy(
            src_ref=router.at[:, :, column(me)],
            dst_ref=router.at[:, :, column(me)],
            send_sem=zero_send.at[k],
            recv_sem=zero_recv.at[k],
            **at("zero", lax.rem(me + k, n)),
        )

    fetch(gate, 0, 0).wait()
    fetch(up, 0, 1).start()
    turn(0, lambda d: send.at[0, d])

    @pl.when(me != 0)
    def _():
        pl.semaphore_wait(barrier, n - 1)
        pl.semaphore_signal(here_sem, inc=1, **at("zero", 0))

    @pl.when(me == 0)
    def _():
        pl.semaphore_wait(here_sem, n - 1)
        for k in range(1, nb):
            pl.semaphore_signal(barrier, inc=1, **at("bank", lax.rem(bank + k, nb)))

    launch(0, 0, 0)

    for copy in router_in:
        copy.wait()
    part[...] = (weight_buf[...] * gain_buf[...]).astype(part.dtype)
    router[bank, :, column(me)] = part[...]

    @pl.loop(0, bulk)
    def _(e):
        for half, source in enumerate((gate, up)):
            t = 2 * e + half
            slot = lax.rem(t, slots)

            def ready():
                fetch(source, e, half).wait()

                @pl.when(t >= slots)
                def _():
                    drain(slot)

                turn(half, lambda d: send.at[slot, d])
                launch(half, e, slot)

            if half == 0:
                pl.when(e > 0)(ready)
            else:
                ready()

            @pl.when(e + 1 < experts)
            def _():
                fetch(source, e + 1, half).start()

        @pl.when((e == min(1, bulk - 1)) & (me == 0))
        def _():
            pl.semaphore_wait(barrier, nb - 1)
            for k in range(1, n):
                pl.semaphore_signal(go_sem, inc=1, **at("zero", k))

        @pl.when(e == min(2, bulk - 1))
        def _():
            @pl.when(me != 0)
            def _():
                pl.semaphore_wait(go_sem, 1)

            for k in range(1, nb):
                bank_copy(k).start()

        @pl.when(e == min(4, bulk - 1))
        def _():
            for k in range(1, nb):
                bank_copy(k).wait()
            for k in range(1, n):
                zero_copy(k).start()

        @pl.when(e >= lag)
        def _():
            settle_both(e - lag)

    @pl.loop(bulk, experts)
    def _(e):
        for half, source in enumerate((gate, up)):
            fetch(source, e, half).wait()
            turn(half, lambda d: late.at[d, half, e - bulk])

            @pl.when(e + 1 < experts)
            def _():
                fetch(source, e + 1, half).start()

    def each_late(act):
        @pl.loop(0, experts - bulk)
        def _(e):
            for half in range(2):
                for k in range(2, n, 2):
                    act(late_copy(half, e, k))

    @pl.loop(bulk - lag, bulk - 1)
    def _(e):
        settle_both(e)

    @pl.when(odd)
    def _():
        each_late(lambda copy: copy.start())

    settle_both(bulk - 1)

    for k in range(1, n):
        zero_copy(k).wait()

    @pl.loop(max(2 * bulk - slots, 0), 2 * bulk)
    def _(t):
        drain(lax.rem(t, slots))

    @pl.when(odd)
    def _():
        each_late(lambda copy: copy.wait())


def cross(
    n, done, late, early, bulk_gate, bulk_up, final, scale_gate, scale_up,
    wide, send_sem, recv_sem, go_sem,
):
    _, _, experts, width, rows = late.shape
    me = lax.axis_index("zero")
    odd = lax.rem(me, 2) == 1
    first = bulk_gate.shape[0] - experts

    def copy(half, e, k):
        peer = lax.rem(me + k, n)
        return pltpu.make_async_remote_copy(
            src_ref=late.at[peer, half, e],
            dst_ref=final.at[me, half, e],
            send_sem=send_sem.at[2 * e + half, k],
            recv_sem=recv_sem.at[2 * e + half, k],
            **at("zero", peer),
        )

    def each(start, act):
        @pl.loop(0, experts)
        def _(e):
            for half in range(2):
                for k in range(start, n, 2):
                    act(copy(half, e, k))

    barrier = pltpu.get_barrier_semaphore()

    @pl.when(jnp.logical_not(odd))
    def _():
        for k in range(2, n, 2):
            pl.semaphore_signal(barrier, inc=1, **at("zero", lax.rem(me + k, n)))
        pl.semaphore_wait(barrier, n // 2 - 1)
        each(2, lambda c: c.start())
        for k in range(1, n, 2):
            pl.semaphore_signal(barrier, inc=1, **at("zero", lax.rem(me + k, n)))

    @pl.when(odd)
    def _():
        pl.semaphore_wait(barrier, n // 2)
        for k in range(1, n, 2):
            pl.semaphore_signal(go_sem, inc=1, **at("zero", lax.rem(me + k, n)))

    def own():
        scale_gate[...] = bulk_gate[...]
        scale_up[...] = bulk_up[...]

        @pl.loop(0, experts)
        def _(e):
            for half in range(2):
                final[me, half, e] = late[me, half, e]

    @pl.when(jnp.logical_not(odd))
    def _():
        own()
        pl.semaphore_wait(go_sem, n // 2)

    each(1, lambda c: c.start())

    @pl.when(odd)
    def _():
        own()

        @pl.loop(0, experts)
        def _(e):
            for half in range(2):
                for k in range(2, n, 2):
                    source = lax.rem(me - k + n, n)
                    final[source, half, e] = early[source // 2, half, e]

    @pl.loop(0, experts)
    def _(e):
        for half, scale in enumerate((scale_gate, scale_up)):

            def block(k):
                return final.at[lax.rem(me - k + n, n), half, e]

            def arrive(k):
                def landed():
                    pltpu.make_async_remote_copy(
                        src_ref=block(k),
                        dst_ref=block(k),
                        send_sem=send_sem.at[0, 0],
                        recv_sem=recv_sem.at[2 * e + half, k],
                        **at("zero", lax.rem(me - k + n, n)),
                    ).wait_recv()

                if k % 2:
                    landed()
                elif k:
                    pl.when(jnp.logical_not(odd))(landed)

            settle(n, block, arrive, wide, scale, first + e)

    each(1, lambda c: c.wait_send())

    @pl.when(jnp.logical_not(odd))
    def _():
        each(2, lambda c: c.wait_send())


def copy_out(source, outs, first, sem):
    n, _, count, _, rows = source.shape
    return [
        pltpu.make_async_copy(
            source.at[s, half],
            out.at[first : first + count, :, s * rows : (s + 1) * rows],
            sem.at[s, half],
        )
        for s in range(n)
        for half, out in enumerate(outs)
    ]


def run(copies):
    for copy in copies:
        copy.start()
    for copy in copies:
        copy.wait()


def finish_bulk(recv, router, ready_gate, ready_up, router_out, done, sem, router_sem):
    done[...] = jnp.zeros_like(done)
    copies = copy_out(recv, (ready_gate, ready_up), 0, sem)
    run(copies + [pltpu.make_async_copy(router, router_out, router_sem)])


def finish_rest(
    final, scale_gate, scale_up, gate_in, up_in, ready_gate, ready_up, scale_gate_out, scale_up_out, sem, scale_sem,
):
    copies = copy_out(final, (ready_gate, ready_up), ready_gate.shape[0] - final.shape[2], sem)
    copies.append(pltpu.make_async_copy(scale_gate, scale_gate_out, scale_sem.at[0]))
    copies.append(pltpu.make_async_copy(scale_up, scale_up_out, scale_sem.at[1]))
    run(copies)


def solution(mesh):
    n, nb = mesh.shape["zero"], mesh.shape["bank"]

    def local(train_gate, train_up, router_weight, router_gain):
        experts, rows, cols = train_gate.shape
        width = cols // n
        d_model = rows * n
        mine = router_weight.shape[1]
        rest = min(max(round(experts * TAIL), 1), experts - 1)
        bulk = experts - rest
        slots = min(SLOTS, 2 * bulk)
        hbm = pl.BlockSpec(memory_space=pltpu.HBM)
        inside = pl.BlockSpec(memory_space=pltpu.VMEM)
        padded = -(-width // LANES) * LANES
        scale = jax.ShapeDtypeStruct((experts, width), jnp.float32)
        joined = jax.ShapeDtypeStruct((nb, mine, d_model), jnp.bfloat16)

        def blocks(sources, count):
            return jax.ShapeDtypeStruct((sources, 2, count, width, rows), jnp.bfloat16)

        recv, router, bulk_gate, bulk_up, late, early = pl.pallas_call(
            functools.partial(exchange, n, nb),
            out_shape=(blocks(n, bulk), joined, scale, scale, blocks(n, rest), blocks(n // 2, rest)),
            in_specs=[hbm] * 4,
            out_specs=(inside,) * 6,
            scratch_shapes=[
                pltpu.VMEM((2, rows, cols), jnp.float32),
                pltpu.VMEM((cols, rows), jnp.float32),
                pltpu.VMEM((slots, n, width, rows), jnp.bfloat16),
                pltpu.VMEM((mine, rows), jnp.bfloat16),
                pltpu.VMEM((padded, LANES), jnp.float32),
                pltpu.VMEM((mine, rows), jnp.float32),
                pltpu.VMEM((1, rows), jnp.float32),
                pltpu.SemaphoreType.DMA((2,)),
                pltpu.SemaphoreType.DMA((2,)),
                pltpu.SemaphoreType.DMA((slots, n)),
                pltpu.SemaphoreType.DMA((2 * bulk, n)),
                pltpu.SemaphoreType.DMA((2 * rest, n)),
                pltpu.SemaphoreType.DMA((2 * rest, n)),
                pltpu.SemaphoreType.DMA((nb,)),
                pltpu.SemaphoreType.DMA((nb,)),
                pltpu.SemaphoreType.DMA((n,)),
                pltpu.SemaphoreType.DMA((n,)),
                pltpu.SemaphoreType.REGULAR,
                pltpu.SemaphoreType.REGULAR,
            ],
            compiler_params=pltpu.CompilerParams(
                collective_id=0, has_side_effects=True, vmem_limit_bytes=EXCHANGE_VMEM
            ),
        )(
            train_gate,
            train_up,
            pltpu.with_memory_space_constraint(router_weight.T, pltpu.HBM),
            pltpu.with_memory_space_constraint(router_gain[None, :], pltpu.HBM),
        )

        ready = jax.ShapeDtypeStruct((experts, width, d_model), jnp.bfloat16)
        ready_gate, ready_up, router, done = pl.pallas_call(
            finish_bulk,
            out_shape=(ready, ready, joined, jax.ShapeDtypeStruct((8, LANES), jnp.float32)),
            in_specs=[inside] * 2,
            out_specs=(hbm,) * 3 + (inside,),
            scratch_shapes=[pltpu.SemaphoreType.DMA((n, 2)), pltpu.SemaphoreType.DMA],
            compiler_params=pltpu.CompilerParams(vmem_limit_bytes=FINISH_VMEM),
        )(recv, router)

        final, scale_gate, scale_up = pl.pallas_call(
            functools.partial(cross, n),
            out_shape=(blocks(n, rest), scale, scale),
            in_specs=[inside] * 5,
            out_specs=(inside,) * 3,
            scratch_shapes=[
                pltpu.VMEM((padded, LANES), jnp.float32),
                pltpu.SemaphoreType.DMA((2 * rest, n)),
                pltpu.SemaphoreType.DMA((2 * rest, n)),
                pltpu.SemaphoreType.REGULAR,
            ],
            compiler_params=pltpu.CompilerParams(
                collective_id=1, has_side_effects=True, vmem_limit_bytes=CROSS_VMEM
            ),
        )(done, late, early, bulk_gate, bulk_up)

        ready_gate, ready_up, scale_gate, scale_up = pl.pallas_call(
            finish_rest,
            out_shape=(ready, ready, scale, scale),
            in_specs=[inside] * 3 + [hbm] * 2,
            out_specs=(hbm,) * 4,
            input_output_aliases={3: 0, 4: 1},
            scratch_shapes=[pltpu.SemaphoreType.DMA((n, 2)), pltpu.SemaphoreType.DMA((2,))],
            compiler_params=pltpu.CompilerParams(vmem_limit_bytes=FINISH_VMEM),
        )(final, scale_gate, scale_up, ready_gate, ready_up)
        return (
            jnp.swapaxes(ready_gate, 1, 2),
            jnp.swapaxes(ready_up, 1, 2),
            scale_gate,
            scale_up,
            router.reshape(nb * mine, d_model).T,
        )

    in_specs = (P("bank", "zero", None), P("bank", "zero", None), P("zero", "bank"), P("zero"))
    out_specs = (
        P("bank", None, "zero"),
        P("bank", None, "zero"),
        P("bank", "zero"),
        P("bank", "zero"),
        P(),
    )
    return jax.shard_map(local, mesh=mesh, in_specs=in_specs, out_specs=out_specs, check_vma=False)
```

time: 270 us -> 264 us (0.978)
  Pallas kernels: 269 us -> 263 us
    pallas_call x2 -> x4, Pallas kernels: 269 us -> 263 us  [the longest x1 225 us: local(): pl.pallas_call(functools.partial(exchange, n, nb), out_shape=(blocks(n, b...]
where the time goes in v2:
time: 264 us; the launch traced here: 263 us
  Pallas kernels  263 us (100%)
    pallas_call x1, Pallas kernels, local(): pl.pallas_call(functools.partial(exchange, n, nb), out_shape=(blocks(n, b...  225 us
    pallas_call x1, Pallas kernels, local(): pl.pallas_call(functools.partial(cross, n), out_shape=(blocks(n, rest), s...  29 us
    pallas_call x1, Pallas kernels, local(): pl.pallas_call(finish_bulk, out_shape=(ready, ready, joined, jax.ShapeDty...  6.62 us

profile of v2, /device:TPU:1, one launch (start us, length us, event | category | flops | bytes accessed | tf_op | source)
XLA Modules:
  0.0 263.2 jit_solution(14703035130885433921)
XLA Ops:
  0.6 224.7 %shard_map.83 = (bf16[8,2,13,176,256]{4,3,2,1,0:T(8,128)(2,1)S(1)}, bf16[4,16,2048]{2,1,0:T(8,128)(2,1)S(1)}, f32[16,176]{1,0:T(8,128)S(1)}, f32[16,176]{1,0:T(8...) custom-call(f32[16,256,1408]{2,1,0:T(8,128)} %gate.1, f32[16,256,1408]{2,1,0:T(8,128)} %up.1, ...), custom_call_target="tpu_custom_call" | custom-call | tf_op jit(solution)/shard_map/pallas_call | solution.py:432
  225.4 6.6 %shard_map.84 = (bf16[16,176,2048]{2,1,0:T(8,128)(2,1)}, bf16[16,176,2048]{2,1,0:T(8,128)(2,1)}, bf16[4,16,2048]{2,1,0:T(8,128)(2,1)}, f32[8,128]{1,0:T(8,128)S(1)}) custom-call(bf16[8,2,13,176,256]{4,3,2,1,0:T(8,128)(2,1)S(1)} %get-tuple-element.22.recv, bf16[4,16,2048]{2,1,0:T(8,128)(2,1)S(1)} %get-tuple-element.23.router), custom_call_target="tpu_custom_call" | custom-call | tf_op jit(solution)/shard_map/pallas_call | solution.py:469
  232.0 29.0 %shard_map.85 = (bf16[8,2,3,176,256]{4,3,2,1,0:T(8,128)(2,1)S(1)}, f32[16,176]{1,0:T(8,128)S(1)}, f32[16,176]{1,0:T(8,128)S(1)}) custom-call(f32[8,128]{1,0:T(8,128)S(1)} %get-tuple-element.24.done, bf16[8,2,3,176,256]{4,3,2,1,0:T(8,128)(2,1)S(1)} %get-tuple-element.25.late, bf16[4,2,3,176,256]{4,3,2,1,0:T(8,128)(2,1)S(1)} %get-tuple-element.26.early, ...), custom_call_target="tpu_custom_call" | custom-call | tf_op jit(solution)/shard_map/pallas_call | solution.py:478
  261.0 2.2 shard_map.86

commit v3 on v2

--- a/solution.py
+++ b/solution.py
@@ -11,7 +11,7 @@
 LANES = 128
 SLOTS = 8
 LAG = 5
-TAIL = 3 / 16
+TAIL = 4 / 16
 EXCHANGE_VMEM = 28 * 2**20
 CROSS_VMEM = 8 * 2**20
 FINISH_VMEM = 2 * 2**20

time: 264 us -> 261 us (0.989)
  Pallas kernels: 263 us -> 260 us
    pallas_call x1, Pallas kernels: 225 us -> 215 us  [local(): pl.pallas_call(functools.partial(exchange, n, nb), out_shape=(blocks(n, b...]
    pallas_call x1, Pallas kernels: 29 us -> 37 us  [local(): pl.pallas_call(functools.partial(cross, n), out_shape=(blocks(n, rest), s...]
where the time goes in v3:
time: 261 us
  Pallas kernels  260 us (100%)
    pallas_call x1, Pallas kernels, local(): pl.pallas_call(functools.partial(exchange, n, nb), out_shape=(blocks(n, b...  215 us
    pallas_call x1, Pallas kernels, local(): pl.pallas_call(functools.partial(cross, n), out_shape=(blocks(n, rest), s...  37 us
    pallas_call x1, Pallas kernels, local(): pl.pallas_call(finish_bulk, out_shape=(ready, ready, joined, jax.ShapeDty...  6.18 us

profile of v3, /device:TPU:1, one launch (start us, length us, event | category | flops | bytes accessed | tf_op | source)
XLA Modules:
  0.0 261.0 jit_solution(2853205366938646155)
XLA Ops:
  0.6 214.6 %shard_map.83 = (bf16[8,2,12,176,256]{4,3,2,1,0:T(8,128)(2,1)S(1)}, bf16[4,16,2048]{2,1,0:T(8,128)(2,1)S(1)}, f32[16,176]{1,0:T(8,128)S(1)}, f32[16,176]{1,0:T(8...) custom-call(f32[16,256,1408]{2,1,0:T(8,128)} %gate.1, f32[16,256,1408]{2,1,0:T(8,128)} %up.1, ...), custom_call_target="tpu_custom_call" | custom-call | tf_op jit(solution)/shard_map/pallas_call | solution.py:432
  215.2 6.2 %shard_map.84 = (bf16[16,176,2048]{2,1,0:T(8,128)(2,1)}, bf16[16,176,2048]{2,1,0:T(8,128)(2,1)}, bf16[4,16,2048]{2,1,0:T(8,128)(2,1)}, f32[8,128]{1,0:T(8,128)S(1)}) custom-call(bf16[8,2,12,176,256]{4,3,2,1,0:T(8,128)(2,1)S(1)} %get-tuple-element.22.recv, bf16[4,16,2048]{2,1,0:T(8,128)(2,1)S(1)} %get-tuple-element.23.router), custom_call_target="tpu_custom_call" | custom-call | tf_op jit(solution)/shard_map/pallas_call | solution.py:469
  221.4 37.0 %shard_map.85 = (bf16[8,2,4,176,256]{4,3,2,1,0:T(8,128)(2,1)S(1)}, f32[16,176]{1,0:T(8,128)S(1)}, f32[16,176]{1,0:T(8,128)S(1)}) custom-call(f32[8,128]{1,0:T(8,128)S(1)} %get-tuple-element.24.done, bf16[8,2,4,176,256]{4,3,2,1,0:T(8,128)(2,1)S(1)} %get-tuple-element.25.late, bf16[4,2,4,176,256]{4,3,2,1,0:T(8,128)(2,1)S(1)} %get-tuple-element.26.early, ...), custom_call_target="tpu_custom_call" | custom-call | tf_op jit(solution)/shard_map/pallas_call | solution.py:478
  258.4 2.7 %shard_map.86 = (bf16[16,176,2048]{2,1,0:T(8,128)(2,1)}, bf16[16,176,2048]{2,1,0:T(8,128)(2,1)}, f32[16,176]{1,0:T(8,128)}, f32[16,176]{1,0:T(8,128)}) custom-call(bf16[8,2,4,176,256]{4,3,2,1,0:T(8,128)(2,1)S(1)} %get-tuple-element.29.final, f32[16,176]{1,0:T(8,128)S(1)} %get-tuple-element.30.scale_gate, ...), custom_call_target="tpu_custom_call", output_to_operand_aliasing={{0}: (3, {}), {1}: (4, {})} | custom-call | tf_op jit(solution)/shard_map/pallas_call | solution.py:494

commit v4 on v3

--- a/solution.py
+++ b/solution.py
@@ -9,7 +9,7 @@
 
 MESH = pl.DeviceIdType.MESH
 LANES = 128
-SLOTS = 8
+SLOTS = 4
 LAG = 5
 TAIL = 4 / 16
 EXCHANGE_VMEM = 28 * 2**20
@@ -57,7 +57,7 @@
 ):
     experts, rows, cols = gate.shape
     width = cols // n
-    bulk = recv.shape[2]
+    bulk = recv.shape[1]
     slots = send.shape[0]
     lag = min(LAG, bulk)
     me = lax.axis_index("zero")
@@ -87,23 +87,23 @@
     scale_gate[...] = jnp.zeros_like(scale_gate)
     scale_up[...] = jnp.zeros_like(scale_up)
 
-    def peer_copy(half, e, slot, k):
+    def peer_copy(e, slot, k, part_of=lambda ref: ref):
         peer = lax.rem(me + k, n)
         return pltpu.make_async_remote_copy(
-            src_ref=send.at[slot, peer],
-            dst_ref=recv.at[me, half, e],
+            src_ref=part_of(send.at[slot, peer]),
+            dst_ref=part_of(recv.at[me, e]),
             send_sem=send_sem.at[slot, k],
-            recv_sem=recv_sem.at[2 * e + half, k],
+            recv_sem=recv_sem.at[e, k],
             **at("zero", peer),
         )
 
-    def late_copy(half, e, k):
+    def late_copy(e, k):
         peer = lax.rem(me + k, n)
         return pltpu.make_async_remote_copy(
-            src_ref=late.at[peer, half, e],
-            dst_ref=early.at[me // 2, half, e],
-            send_sem=late_send.at[2 * e + half, k],
-            recv_sem=late_recv.at[2 * e + half, k],
+            src_ref=late.at[peer, e],
+            dst_ref=early.at[me // 2, e],
+            send_sem=late_send.at[e, k],
+            recv_sem=late_recv.at[e, k],
             **at("zero", peer),
         )
 
@@ -115,27 +115,31 @@
 
     def drain(slot):
         for k in range(1, n):
-            peer_copy(0, 0, slot, k).wait_send()
-
-    def launch(half, e, slot):
+            peer_copy(0, slot, k).wait_send()
+
+    def launch(e, slot, half=None):
+        def part_of(ref):
+            return ref if half is None else ref.at[half]
+
         for k in range(1, n):
-            peer_copy(half, e, slot, k).start()
-        recv[me, half, e] = send[slot, me]
+            peer_copy(e, slot, k, part_of).start()
+        part_of(recv.at[me, e])[...] = part_of(send.at[slot, me])[...]
 
     def settle_both(e):
         for half, scale in enumerate((scale_gate, scale_up)):
 
             def block(k):
-                return recv.at[lax.rem(me - k + n, n), half, e]
+                return recv.at[lax.rem(me - k + n, n), e, half]
 
             def arrive(k):
-                if k > 0:
+                if k > 0 and half == 0:
+                    source = lax.rem(me - k + n, n)
                     pltpu.make_async_remote_copy(
-                        src_ref=block(k),
-                        dst_ref=block(k),
+                        src_ref=recv.at[source, e],
+                        dst_ref=recv.at[source, e],
                         send_sem=send_sem.at[0, 0],
-                        recv_sem=recv_sem.at[2 * e + half, k],
-                        **at("zero", lax.rem(me - k + n, n)),
+                        recv_sem=recv_sem.at[e, k],
+                        **at("zero", source),
                     ).wait_recv()
 
             settle(n, block, arrive, wide, scale, e)
@@ -163,7 +167,8 @@
 
     fetch(gate, 0, 0).wait()
     fetch(up, 0, 1).start()
-    turn(0, lambda d: send.at[0, d])
+    turn(0, lambda d: send.at[0, d, 0])
+    fetch(gate, 1, 0).start()
 
     @pl.when(me != 0)
     def _():
@@ -177,36 +182,34 @@
             pl.semaphore_signal(barrier, inc=1, **at("bank", lax.rem(bank + k, nb)))
 
     launch(0, 0, 0)
+
+    fetch(up, 0, 1).wait()
+    turn(1, lambda d: send.at[0, d, 1])
+    fetch(up, 1, 1).start()
+    launch(0, 0, 1)
 
     for copy in router_in:
         copy.wait()
     part[...] = (weight_buf[...] * gain_buf[...]).astype(part.dtype)
     router[bank, :, column(me)] = part[...]
 
-    @pl.loop(0, bulk)
+    @pl.loop(1, bulk)
     def _(e):
+        slot = lax.rem(e, slots)
+
+        @pl.when(e >= slots)
+        def _():
+            drain(slot)
+
         for half, source in enumerate((gate, up)):
-            t = 2 * e + half
-            slot = lax.rem(t, slots)
-
-            def ready():
-                fetch(source, e, half).wait()
-
-                @pl.when(t >= slots)
-                def _():
-                    drain(slot)
-
-                turn(half, lambda d: send.at[slot, d])
-                launch(half, e, slot)
-
-            if half == 0:
-                pl.when(e > 0)(ready)
-            else:
-                ready()
+            fetch(source, e, half).wait()
+            turn(half, lambda d: send.at[slot, d, half])
 
             @pl.when(e + 1 < experts)
             def _():
                 fetch(source, e + 1, half).start()
+
+        launch(e, slot)
 
         @pl.when((e == min(1, bulk - 1)) & (me == 0))
         def _():
@@ -238,7 +241,7 @@
     def _(e):
         for half, source in enumerate((gate, up)):
             fetch(source, e, half).wait()
-            turn(half, lambda d: late.at[d, half, e - bulk])
+            turn(half, lambda d: late.at[d, e - bulk, half])
 
             @pl.when(e + 1 < experts)
             def _():
@@ -247,9 +250,8 @@
     def each_late(act):
         @pl.loop(0, experts - bulk)
         def _(e):
-            for half in range(2):
-                for k in range(2, n, 2):
-                    act(late_copy(half, e, k))
+            for k in range(2, n, 2):
+                act(late_copy(e, k))
 
     @pl.loop(bulk - lag, bulk - 1)
     def _(e):
@@ -264,9 +266,9 @@
     for k in range(1, n):
         zero_copy(k).wait()
 
-    @pl.loop(max(2 * bulk - slots, 0), 2 * bulk)
-    def _(t):
-        drain(lax.rem(t, slots))
+    @pl.loop(bulk - slots, bulk)
+    def _(e):
+        drain(lax.rem(e, slots))
 
     @pl.when(odd)
     def _():
@@ -277,27 +279,64 @@
     n, done, late, early, bulk_gate, bulk_up, final, scale_gate, scale_up,
     wide, send_sem, recv_sem, go_sem,
 ):
-    _, _, experts, width, rows = late.shape
+    experts = late.shape[1]
     me = lax.axis_index("zero")
     odd = lax.rem(me, 2) == 1
     first = bulk_gate.shape[0] - experts
 
-    def copy(half, e, k):
+    last = experts - 1
+
+    def copy(e, k, half=None):
         peer = lax.rem(me + k, n)
+        row = e if half is None else e + half
+
+        def part_of(ref):
+            return ref if half is None else ref.at[half]
+
         return pltpu.make_async_remote_copy(
-            src_ref=late.at[peer, half, e],
-            dst_ref=final.at[me, half, e],
-            send_sem=send_sem.at[2 * e + half, k],
-            recv_sem=recv_sem.at[2 * e + half, k],
+            src_ref=part_of(late.at[peer, e]),
+            dst_ref=part_of(final.at[me, e]),
+            send_sem=send_sem.at[row, k],
+            recv_sem=recv_sem.at[row, k],
             **at("zero", peer),
         )
 
     def each(start, act):
-        @pl.loop(0, experts)
+        @pl.loop(0, last)
         def _(e):
-            for half in range(2):
-                for k in range(start, n, 2):
-                    act(copy(half, e, k))
+            for k in range(start, n, 2):
+                act(copy(e, k))
+
+        for half in range(2):
+            for k in range(start, n, 2):
+                act(copy(last, k, half))
+
+    def step(e, halves):
+        for half, scale in enumerate((scale_gate, scale_up)):
+
+            def block(k):
+                return final.at[lax.rem(me - k + n, n), e, half]
+
+            def arrive(k):
+                source = lax.rem(me - k + n, n)
+                arrived = block(k) if halves else final.at[source, e]
+
+                def landed():
+                    pltpu.make_async_remote_copy(
+                        src_ref=arrived,
+                        dst_ref=arrived,
+                        send_sem=send_sem.at[0, 0],
+                        recv_sem=recv_sem.at[e + half, k],
+                        **at("zero", source),
+                    ).wait_recv()
+
+                if halves or half == 0:
+                    if k % 2:
+                        landed()
+                    elif k:
+                        pl.when(jnp.logical_not(odd))(landed)
+
+            settle(n, block, arrive, wide, scale, first + e)
 
     barrier = pltpu.get_barrier_semaphore()
 
@@ -322,50 +361,30 @@
 
         @pl.loop(0, experts)
         def _(e):
-            for half in range(2):
-                final[me, half, e] = late[me, half, e]
+            final[me, e] = late[me, e]
 
     @pl.when(jnp.logical_not(odd))
     def _():
         own()
         pl.semaphore_wait(go_sem, n // 2)
 
-    each(1, lambda c: c.start())
-
     @pl.when(odd)
     def _():
         own()
 
         @pl.loop(0, experts)
         def _(e):
-            for half in range(2):
-                for k in range(2, n, 2):
-                    source = lax.rem(me - k + n, n)
-                    final[source, half, e] = early[source // 2, half, e]
-
-    @pl.loop(0, experts)
+            for k in range(2, n, 2):
+                source = lax.rem(me - k + n, n)
+                final[source, e] = early[source // 2, e]
+
+    each(1, lambda c: c.start())
+
+    @pl.loop(0, last)
     def _(e):
-        for half, scale in enumerate((scale_gate, scale_up)):
-
-            def block(k):
-                return final.at[lax.rem(me - k + n, n), half, e]
-
-            def arrive(k):
-                def landed():
-                    pltpu.make_async_remote_copy(
-                        src_ref=block(k),
-                        dst_ref=block(k),
-                        send_sem=send_sem.at[0, 0],
-                        recv_sem=recv_sem.at[2 * e + half, k],
-                        **at("zero", lax.rem(me - k + n, n)),
-                    ).wait_recv()
-
-                if k % 2:
-                    landed()
-                elif k:
-                    pl.when(jnp.logical_not(odd))(landed)
-
-            settle(n, block, arrive, wide, scale, first + e)
+        step(e, False)
+
+    step(last, True)
 
     each(1, lambda c: c.wait_send())
 
@@ -375,10 +394,10 @@
 
 
 def copy_out(source, outs, first, sem):
-    n, _, count, _, rows = source.shape
+    n, count, _, _, rows = source.shape
     return [
         pltpu.make_async_copy(
-            source.at[s, half],
+            source.at[s, :, half],
             out.at[first : first + count, :, s * rows : (s + 1) * rows],
             sem.at[s, half],
         )
@@ -403,7 +422,7 @@
 def finish_rest(
     final, scale_gate, scale_up, gate_in, up_in, ready_gate, ready_up, scale_gate_out, scale_up_out, sem, scale_sem,
 ):
-    copies = copy_out(final, (ready_gate, ready_up), ready_gate.shape[0] - final.shape[2], sem)
+    copies = copy_out(final, (ready_gate, ready_up), ready_gate.shape[0] - final.shape[1], sem)
     copies.append(pltpu.make_async_copy(scale_gate, scale_gate_out, scale_sem.at[0]))
     copies.append(pltpu.make_async_copy(scale_up, scale_up_out, scale_sem.at[1]))
     run(copies)
@@ -419,7 +438,7 @@
         mine = router_weight.shape[1]
         rest = min(max(round(experts * TAIL), 1), experts - 1)
         bulk = experts - rest
-        slots = min(SLOTS, 2 * bulk)
+        slots = min(SLOTS, bulk)
         hbm = pl.BlockSpec(memory_space=pltpu.HBM)
         inside = pl.BlockSpec(memory_space=pltpu.VMEM)
         padded = -(-width // LANES) * LANES
@@ -427,7 +446,7 @@
         joined = jax.ShapeDtypeStruct((nb, mine, d_model), jnp.bfloat16)
 
         def blocks(sources, count):
-            return jax.ShapeDtypeStruct((sources, 2, count, width, rows), jnp.bfloat16)
+            return jax.ShapeDtypeStruct((sources, count, 2, width, rows), jnp.bfloat16)
 
         recv, router, bulk_gate, bulk_up, late, early = pl.pallas_call(
             functools.partial(exchange, n, nb),
@@ -437,7 +456,7 @@
             scratch_shapes=[
                 pltpu.VMEM((2, rows, cols), jnp.float32),
                 pltpu.VMEM((cols, rows), jnp.float32),
-                pltpu.VMEM((slots, n, width, rows), jnp.bfloat16),
+                pltpu.VMEM((slots, n, 2, width, rows), jnp.bfloat16),
                 pltpu.VMEM((mine, rows), jnp.bfloat16),
                 pltpu.VMEM((padded, LANES), jnp.float32),
                 pltpu.VMEM((mine, rows), jnp.float32),
@@ -445,9 +464,9 @@
                 pltpu.SemaphoreType.DMA((2,)),
                 pltpu.SemaphoreType.DMA((2,)),
                 pltpu.SemaphoreType.DMA((slots, n)),
-                pltpu.SemaphoreType.DMA((2 * bulk, n)),
-                pltpu.SemaphoreType.DMA((2 * rest, n)),
-                pltpu.SemaphoreType.DMA((2 * rest, n)),
+                pltpu.SemaphoreType.DMA((bulk, n)),
+                pltpu.SemaphoreType.DMA((rest, n)),
+                pltpu.SemaphoreType.DMA((rest, n)),
                 pltpu.SemaphoreType.DMA((nb,)),
                 pltpu.SemaphoreType.DMA((nb,)),
                 pltpu.SemaphoreType.DMA((n,)),
@@ -482,8 +501,8 @@
             out_specs=(inside,) * 3,
             scratch_shapes=[
                 pltpu.VMEM((padded, LANES), jnp.float32),
-                pltpu.SemaphoreType.DMA((2 * rest, n)),
-                pltpu.SemaphoreType.DMA((2 * rest, n)),
+                pltpu.SemaphoreType.DMA((rest + 1, n)),
+                pltpu.SemaphoreType.DMA((rest + 1, n)),
                 pltpu.SemaphoreType.REGULAR,
             ],
             compiler_params=pltpu.CompilerParams(

time: 261 us -> 260 us (level)
  no operation moved by 1% of the time
where the time goes in v4:
time: 260 us
  Pallas kernels  259 us (100%)
    pallas_call x1, Pallas kernels, local(): pl.pallas_call(functools.partial(exchange, n, nb), out_shape=(blocks(n, b...  214 us
    pallas_call x1, Pallas kernels, local(): pl.pallas_call(functools.partial(cross, n), out_shape=(blocks(n, rest), s...  36.6 us
    pallas_call x1, Pallas kernels, local(): pl.pallas_call(finish_bulk, out_shape=(ready, ready, joined, jax.ShapeDty...  6.18 us

profile of v4, /device:TPU:1, one launch (start us, length us, event | category | flops | bytes accessed | tf_op | source)
XLA Modules:
  0.0 260.1 jit_solution(18435389840099381046)
XLA Ops:
  0.6 214.1 %shard_map.83 = (bf16[8,12,2,176,256]{4,3,2,1,0:T(8,128)(2,1)S(1)}, bf16[4,16,2048]{2,1,0:T(8,128)(2,1)S(1)}, f32[16,176]{1,0:T(8,128)S(1)}, f32[16,176]{1,0:T(8...) custom-call(f32[16,256,1408]{2,1,0:T(8,128)} %gate.1, f32[16,256,1408]{2,1,0:T(8,128)} %up.1, ...), custom_call_target="tpu_custom_call" | custom-call | tf_op jit(solution)/shard_map/pallas_call | solution.py:451
  214.7 6.2 %shard_map.84 = (bf16[16,176,2048]{2,1,0:T(8,128)(2,1)}, bf16[16,176,2048]{2,1,0:T(8,128)(2,1)}, bf16[4,16,2048]{2,1,0:T(8,128)(2,1)}, f32[8,128]{1,0:T(8,128)S(1)}) custom-call(bf16[8,12,2,176,256]{4,3,2,1,0:T(8,128)(2,1)S(1)} %get-tuple-element.22.recv, bf16[4,16,2048]{2,1,0:T(8,128)(2,1)S(1)} %get-tuple-element.23.router), custom_call_target="tpu_custom_call" | custom-call | tf_op jit(solution)/shard_map/pallas_call | solution.py:488
  220.9 36.6 %shard_map.85 = (bf16[8,4,2,176,256]{4,3,2,1,0:T(8,128)(2,1)S(1)}, f32[16,176]{1,0:T(8,128)S(1)}, f32[16,176]{1,0:T(8,128)S(1)}) custom-call(f32[8,128]{1,0:T(8,128)S(1)} %get-tuple-element.24.done, bf16[8,4,2,176,256]{4,3,2,1,0:T(8,128)(2,1)S(1)} %get-tuple-element.25.late, bf16[4,4,2,176,256]{4,3,2,1,0:T(8,128)(2,1)S(1)} %get-tuple-element.26.early, ...), custom_call_target="tpu_custom_call" | custom-call | tf_op jit(solution)/shard_map/pallas_call | solution.py:497
  257.5 2.7 %shard_map.86 = (bf16[16,176,2048]{2,1,0:T(8,128)(2,1)}, bf16[16,176,2048]{2,1,0:T(8,128)(2,1)}, f32[16,176]{1,0:T(8,128)}, f32[16,176]{1,0:T(8,128)}) custom-call(bf16[8,4,2,176,256]{4,3,2,1,0:T(8,128)(2,1)S(1)} %get-tuple-element.29.final, f32[16,176]{1,0:T(8,128)S(1)} %get-tuple-element.30.scale_gate, ...), custom_call_target="tpu_custom_call", output_to_operand_aliasing={{0}: (3, {}), {1}: (4, {})} | custom-call | tf_op jit(solution)/shard_map/pallas_call | solution.py:513

commit v5 on v4

--- a/solution.py
+++ b/solution.py
@@ -279,13 +279,16 @@
     n, done, late, early, bulk_gate, bulk_up, final, scale_gate, scale_up,
     wide, send_sem, recv_sem, go_sem,
 ):
-    experts = late.shape[1]
+    experts, rows = late.shape[1], late.shape[4]
     me = lax.axis_index("zero")
     odd = lax.rem(me, 2) == 1
     first = bulk_gate.shape[0] - experts
 
     last = experts - 1
 
+    def place(source, e):
+        return final.at[e, :, :, pl.ds(pl.multiple_of(source * rows, rows), rows)]
+
     def copy(e, k, half=None):
         peer = lax.rem(me + k, n)
         row = e if half is None else e + half
@@ -295,7 +298,7 @@
 
         return pltpu.make_async_remote_copy(
             src_ref=part_of(late.at[peer, e]),
-            dst_ref=part_of(final.at[me, e]),
+            dst_ref=part_of(place(me, e)),
             send_sem=send_sem.at[row, k],
             recv_sem=recv_sem.at[row, k],
             **at("zero", peer),
@@ -315,11 +318,11 @@
         for half, scale in enumerate((scale_gate, scale_up)):
 
             def block(k):
-                return final.at[lax.rem(me - k + n, n), e, half]
+                return place(lax.rem(me - k + n, n), e).at[half]
 
             def arrive(k):
                 source = lax.rem(me - k + n, n)
-                arrived = block(k) if halves else final.at[source, e]
+                arrived = block(k) if halves else place(source, e)
 
                 def landed():
                     pltpu.make_async_remote_copy(
@@ -361,7 +364,7 @@
 
         @pl.loop(0, experts)
         def _(e):
-            final[me, e] = late[me, e]
+            place(me, e)[...] = late[me, e]
 
     @pl.when(jnp.logical_not(odd))
     def _():
@@ -376,7 +379,7 @@
         def _(e):
             for k in range(2, n, 2):
                 source = lax.rem(me - k + n, n)
-                final[source, e] = early[source // 2, e]
+                place(source, e)[...] = early[source // 2, e]
 
     each(1, lambda c: c.start())
 
@@ -422,7 +425,13 @@
 def finish_rest(
     final, scale_gate, scale_up, gate_in, up_in, ready_gate, ready_up, scale_gate_out, scale_up_out, sem, scale_sem,
 ):
-    copies = copy_out(final, (ready_gate, ready_up), ready_gate.shape[0] - final.shape[1], sem)
+    count = final.shape[0]
+    first = ready_gate.shape[0] - count
+    copies = [
+        pltpu.make_async_copy(final.at[e, half], out.at[first + e], sem.at[e, half])
+        for e in range(count)
+        for half, out in enumerate((ready_gate, ready_up))
+    ]
     copies.append(pltpu.make_async_copy(scale_gate, scale_gate_out, scale_sem.at[0]))
     copies.append(pltpu.make_async_copy(scale_up, scale_up_out, scale_sem.at[1]))
     run(copies)
@@ -496,7 +505,7 @@
 
         final, scale_gate, scale_up = pl.pallas_call(
             functools.partial(cross, n),
-            out_shape=(blocks(n, rest), scale, scale),
+            out_shape=(jax.ShapeDtypeStruct((rest, 2, width, d_model), jnp.bfloat16), scale, scale),
             in_specs=[inside] * 5,
             out_specs=(inside,) * 3,
             scratch_shapes=[
@@ -516,7 +525,7 @@
             in_specs=[inside] * 3 + [hbm] * 2,
             out_specs=(hbm,) * 4,
             input_output_aliases={3: 0, 4: 1},
-            scratch_shapes=[pltpu.SemaphoreType.DMA((n, 2)), pltpu.SemaphoreType.DMA((2,))],
+            scratch_shapes=[pltpu.SemaphoreType.DMA((rest, 2)), pltpu.SemaphoreType.DMA((2,))],
             compiler_params=pltpu.CompilerParams(vmem_limit_bytes=FINISH_VMEM),
         )(final, scale_gate, scale_up, ready_gate, ready_up)
         return (

time: 260 us -> 261 us (level)
  no operation moved by 1% of the time
where the time goes in v5:
time: 261 us; the launch traced here: 260 us
  Pallas kernels  260 us (100%)
    pallas_call x1, Pallas kernels, local(): pl.pallas_call(functools.partial(exchange, n, nb), out_shape=(blocks(n, b...  214 us
    pallas_call x1, Pallas kernels, local(): pl.pallas_call(functools.partial(cross, n), out_shape=(jax.ShapeDtypeStru...  36.7 us
    pallas_call x1, Pallas kernels, local(): pl.pallas_call(finish_bulk, out_shape=(ready, ready, joined, jax.ShapeDty...  6.18 us

profile of v5, /device:TPU:1, one launch (start us, length us, event | category | flops | bytes accessed | tf_op | source)
XLA Modules:
  0.0 260.2 jit_solution(627351244490685201)
XLA Ops:
  0.6 214.1 %shard_map.83 = (bf16[8,12,2,176,256]{4,3,2,1,0:T(8,128)(2,1)S(1)}, bf16[4,16,2048]{2,1,0:T(8,128)(2,1)S(1)}, f32[16,176]{1,0:T(8,128)S(1)}, f32[16,176]{1,0:T(8...) custom-call(f32[16,256,1408]{2,1,0:T(8,128)} %gate.1, f32[16,256,1408]{2,1,0:T(8,128)} %up.1, ...), custom_call_target="tpu_custom_call" | custom-call | tf_op jit(solution)/shard_map/pallas_call | solution.py:460
  214.7 6.2 %shard_map.84 = (bf16[16,176,2048]{2,1,0:T(8,128)(2,1)}, bf16[16,176,2048]{2,1,0:T(8,128)(2,1)}, bf16[4,16,2048]{2,1,0:T(8,128)(2,1)}, f32[8,128]{1,0:T(8,128)S(1)}) custom-call(bf16[8,12,2,176,256]{4,3,2,1,0:T(8,128)(2,1)S(1)} %get-tuple-element.22.recv, bf16[4,16,2048]{2,1,0:T(8,128)(2,1)S(1)} %get-tuple-element.23.router), custom_call_target="tpu_custom_call" | custom-call | tf_op jit(solution)/shard_map/pallas_call | solution.py:497
  220.9 36.7 %shard_map.85 = (bf16[4,2,176,2048]{3,2,1,0:T(8,128)(2,1)S(1)}, f32[16,176]{1,0:T(8,128)S(1)}, f32[16,176]{1,0:T(8,128)S(1)}) custom-call(f32[8,128]{1,0:T(8,128)S(1)} %get-tuple-element.24.done, bf16[8,4,2,176,256]{4,3,2,1,0:T(8,128)(2,1)S(1)} %get-tuple-element.25.late, bf16[4,4,2,176,256]{4,3,2,1,0:T(8,128)(2,1)S(1)} %get-tuple-element.26.early, ...), custom_call_target="tpu_custom_call" | custom-call | tf_op jit(solution)/shard_map/pallas_call | solution.py:506
  257.6 2.6 shard_map.86
